TPU v7x, 128 devices: a whole 4x4x4 slice. The times are simulated.
128 devices in a mesh: scen: 32 (over z, y_lo, x), fac: 4 (over y_hi, core).
Axes of the slice: x: 4, y: 4 (y_hi: 2, y_lo: 2; y = y_hi * 2 + y_lo), z: 4, core: 2. Of those that a mesh axis runs over, the one named last changes fastest.
Arguments:
- scenario_draws: bfloat16 [32768, 4096], P('scen'), may hold values from -6 to 6
- cholesky: bfloat16 [4096, 4096], P('scen', 'fac'), may hold values from -1.5 to 1.5, as said below
- exposures: bfloat16 [4096, 4096], P('fac'), may hold values from -0.09375 to 0.09375
- drift: float32 [4096], P('fac'), may hold values from -3 to 3
Outputs:
- covariance: float32 [4096, 4096], P('scen', 'fac')
- expected: float32 [4096], P('fac')
Inputs may be any that keep to these rules, and one draw needn't show every extreme that they name: cholesky is lower triangular (zero above the diagonal) with diagonal entries of 0.5 to 1.5.
All inputs are finite; a program needn't handle non-finite values.
Results may differ from a plain program's by a relative error of at most 0.0013.
Values may be sent and summed in bfloat16 or wider, within the bound.
No kernel may reach another device: no remote copies, remote signals or barrier semaphores. Data moves between devices by JAX's collectives and lax.ppermute only.
A program may use at most 128 MiB of HBM per device.

v0:
```python
import jax
import jax.numpy as jnp
from jax import lax
from jax.sharding import Mesh
from jax.sharding import PartitionSpec as P

SCEN = ("scen_0", "scen_1", "scen_2")


def in_order(tiles, dim):
    tiles = jnp.moveaxis(tiles, 0, dim)
    shape = tiles.shape
    return tiles.reshape(*shape[:dim], shape[dim] * shape[dim + 1], *shape[dim + 2 :])


def gather_in_order(x, axes, order):
    tiles = x
    for k in order:
        tiles = lax.all_gather(tiles, axes[k])
    done = order[::-1]
    back = [done.index(k) for k in range(len(axes))]
    tiles = tiles.transpose(*back, *range(len(axes), tiles.ndim))
    return tiles.reshape(-1, *x.shape)


def whole_of(x, axes, order, dim):
    return in_order(gather_in_order(x, axes, order), dim)


def from_everyone(x, axis):
    copies = jnp.broadcast_to(x, (lax.axis_size(axis), *x.shape))
    return lax.all_to_all(copies, axis, split_axis=0, concat_axis=0, tiled=True)


def over_copies(x, axis):
    return from_everyone(x, axis).sum(axis=0)


def on_device(scenario_draws, cholesky, exposures, drift):
    count_rows = scenario_draws.shape[0]
    own_desks = exposures.shape[0]
    mixed = jnp.dot(
        scenario_draws, whole_of(cholesky, SCEN, (1, 0, 2), 0), preferred_element_type=jnp.float32
    )
    shocks = (mixed + drift[None, :]).astype(jnp.bfloat16)
    pnl_acc = lax.dot_general(
        lax.all_gather(shocks, "fac", axis=1, tiled=True),
        exposures,
        (((1,), (1,)), ((), ())),
        preferred_element_type=jnp.float32,
    )
    pnl = pnl_acc.astype(jnp.bfloat16)
    gathered = lax.all_gather(pnl, "fac", axis=1, tiled=True)
    desk_total = gathered.shape[1]
    column_sums = over_copies(jnp.sum(gathered, axis=0, dtype=jnp.float32), SCEN)
    scenario_total = count_rows * lax.axis_size(SCEN)
    means = column_sums / scenario_total
    col_means = lax.dynamic_slice_in_dim(means, lax.axis_index("fac") * own_desks, own_desks, 0)
    owned_rows = desk_total // lax.axis_size(SCEN)
    row_start = lax.axis_index(SCEN) * owned_rows
    block = lax.psum_scatter(
        lax.dot_general(
            gathered, pnl, (((0,), (0,)), ((), ())), preferred_element_type=jnp.float32
        ),
        SCEN,
        scatter_dimension=0,
        tiled=True,
    )
    row_means = lax.dynamic_slice_in_dim(means, row_start, owned_rows, 0)
    covariance = (block - scenario_total * row_means[:, None] * col_means[None, :]) / (
        scenario_total - 1
    )
    return (covariance, col_means)


def solution(mesh):
    torus = Mesh(
        mesh.devices.reshape(4, 2, 4, mesh.shape["fac"]), ("scen_0", "scen_1", "scen_2", "fac")
    )
    in_specs = (P(SCEN, None), P(SCEN, "fac"), P("fac", None), P("fac"))
    out_specs = (P(SCEN, "fac"), P("fac"))
    return jax.shard_map(
        on_device, mesh=torus, in_specs=in_specs, out_specs=out_specs, check_vma=False
    )
```

profile of v0, /device:TPU:0, one launch (start us, length us, event | category | flops | bytes accessed | tf_op | source)
XLA Modules:
  0.0 532.6 jit_solution(352595188754719642)
XLA Ops:
  7.2 0.0 all-gather.12.cloned.1.call-start
  7.2 10.6 %all-gather = bf16[256,1024]{1,0:T(8,128)(2,1)} all-gather(bf16[128,1024]{1,0:T(8,128)(2,1)} %param.5), channel_id=2, replica_groups=mesh['scen_0'=4,'scen_1'=2,'scen_2'=4,'fac'=4] {'scen_1'}, dimensions={0}, use_global_device_ids=true | all-gather | bytes 786432 | tf_op jit(solution)/shard_map/all_gather | solution.py:19
  17.8 0.0 all-gather.12.cloned.1.call-update
  17.9 0.0 all-gather.14.cloned.1.call-start
  17.9 33.2 %all-gather.12.cloned.1.call-done = bf16[8,128,1024]{2,1,0:T(8,128)(2,1)} async-done(((bf16[2,128,1024]{2,1,0:T(8,128)(2,1)}), bf16[8,128,1024]{2,1,0:T(8,128)(2,1)}) %all-gather.12.cloned.1.call-update) | async-done | bytes 2097168 | tf_op jit(solution)/shard_map/all_gather | solution.py:19
  51.1 0.0 all-gather.14.cloned.1.call-update
  51.1 0.0 all-gather.8.cloned.1.call-start
  51.2 84.5 %all-gather.14.cloned.1.call-done = bf16[16,2,128,1024]{3,2,1,0:T(8,128)(2,1)} async-done(((bf16[4,2,128,1024]{3,2,1,0:T(8,128)(2,1)}), bf16[16,2,128,1024]{3,2,1,0:T(8,128)(2,1)}) %all-gather.14.cloned.1.call-update) | async-done | bytes 8388624 | tf_op jit(solution)/shard_map/all_gather | solution.py:19
  135.7 0.0 copy-start.1
  135.7 8.2 %copy.9 = bf16[4,2,4,128,1024]{4,3,2,1,0:T(8,128)(2,1)} copy(bf16[4,2,4,128,1024]{4,3,1,0,2:T(8,128)(2,1)} %bitcast.12) | data formatting | bytes 16777216 | tf_op jit(solution)/shard_map/transpose | solution.py:22
  143.9 0.0 copy-done.1
  143.9 14.7 %add_convert_fusion = bf16[1024,1024]{1,0:T(8,128)(2,1)} fusion(f32[1024]{0:T(1024)S(1)} %copy-done.1, bf16[1024,4096]{1,0:T(8,128)(2,1)} %param.4, bf16[4096,1024]{1,0:T(8,128)(2,1)} %bitcast.13), kind=kOutput, calls=%fused_computation.1 | convolution fusion | flops 8592031744 | bytes 18878464 | tf_op jit(solution)/shard_map/dot_general | solution.py:42
  158.6 0.0 all-gather.8.cloned.1.call-update
  158.7 0.0 all-gather.10.cloned.1.call-start
  158.7 63.4 %all-gather.8.cloned.1.call-done = bf16[1024,4096]{1,0:T(8,128)(2,1)} async-done(((bf16[1024,1024]{1,0:T(8,128)(2,1)}), bf16[1024,4096]{1,0:T(8,128)(2,1)}) %all-gather.8.cloned.1.call-update) | async-done | bytes 8388624 | tf_op jit(solution)/shard_map/all_gather | solution.py:47
  222.1 14.8 %convolution_convert_fusion = bf16[1024,1024]{1,0:T(8,128)(2,1)} fusion(bf16[1024,4096]{1,0:T(8,128)(2,1)} %all-gather.8.cloned.1.call-done, bf16[1024,4096]{1,0:T(8,128)(2,1)} %param.6), kind=kOutput, calls=%fused_computation.2 | convolution fusion | flops 8590983168 | bytes 18874368 | tf_op jit(solution)/shard_map/dot_general | solution.py:46
  236.9 0.0 all-gather.10.cloned.1.call-update
  236.9 0.2 reduce-scatter.2.cloned.1.call-start
  237.1 61.6 %all-gather.10.cloned.1.call-done = bf16[1024,4096]{1,0:T(8,128)(2,1)} async-done(((bf16[1024,1024]{1,0:T(8,128)(2,1)}), bf16[1024,4096]{1,0:T(8,128)(2,1)}) %all-gather.10.cloned.1.call-update) | async-done | bytes 8388624 | tf_op jit(solution)/shard_map/all_gather | solution.py:53
  298.8 16.1 %fusion = f32[4096,1024]{1,0:T(8,128)} fusion(bf16[1024,4096]{1,0:T(8,128)(2,1)} %all-gather.10.cloned.1.call-done, bf16[1024,1024]{1,0:T(8,128)(2,1)} %convolution_convert_fusion), kind=kOutput, calls=%fused_computation.6 | convolution fusion | flops 8589934592 | bytes 27262976 | tf_op jit(solution)/shard_map/dot_general | solution.py:62
  314.9 0.0 reduce-scatter.2.cloned.1.call-update
  314.9 4.6 convert_reduce_fusion
  319.5 1.3 broadcast_in_dim.2
  320.7 7.3 %all-to-all-start = ((f32[32,1,4096]{2,1,0:T(1,128)}), f32[32,1,4096]{2,1,0:T(1,128)S(1)}, u32[]{:S(2)}, u32[]{:S(2)}) async-start(f32[32,1,4096]{2,1,0:T(1,128)} %broadcast_in_dim.2), calls=%async_computation.1 | async-start | bytes 1048576 | tf_op jit(solution)/shard_map/all_to_all | solution.py:32
  328.0 17.8 %all-to-all-done = f32[32,1,4096]{2,1,0:T(1,128)S(1)} async-done(((f32[32,1,4096]{2,1,0:T(1,128)}), f32[32,1,4096]{2,1,0:T(1,128)S(1)}, u32[]{:S(2)}, u32[]{:S(2)}) %all-to-all-start) | async-done | bytes 524320 | tf_op jit(solution)/shard_map/all_to_all | solution.py:32
  345.8 0.4 reduce_sum.19
  346.2 0.0 copy-start
  346.2 0.1 dynamic-slice_multiply_fusion
  346.3 177.8 %reduce-scatter.2.cloned.1.call-done = f32[128,1024]{1,0:T(8,128)} async-done(((f32[4096,1024]{1,0:T(8,128)}), f32[128,1024]{1,0:T(8,128)}) %reduce-scatter.2.cloned.1.call-update) | async-done | bytes 524304 | tf_op jit(solution)/shard_map/reduce_scatter | solution.py:61
  524.1 2.0 subtract_multiply_fusion
  526.0 0.0 copy-done
  (2 shorter events, 0.0 us)
Async XLA Ops:
  7.2 43.9 %all-gather.12.cloned.1.call-start = ((), (), s32[]{:S(2)}) async-start(), calls=%async_computation.5 | async-start | bytes 2621440 | tf_op jit(solution)/shard_map/all_gather | solution.py:19
  17.9 117.8 %all-gather.14.cloned.1.call-start = ((), (), s32[]{:S(2)}) async-start(), calls=%async_computation.6 | async-start | bytes 10485760 | tf_op jit(solution)/shard_map/all_gather | solution.py:19
  51.1 171.0 %all-gather.8.cloned.1.call-start = ((), (), s32[]{:S(2)}) async-start(), calls=%async_computation.2 | async-start | bytes 10485760 | tf_op jit(solution)/shard_map/all_gather | solution.py:47
  135.7 8.2 %copy-start.1 = (f32[1024]{0:T(1024)S(1)}, f32[1024]{0:T(1024)}, u32[]{:S(2)}) copy-start(f32[1024]{0:T(1024)} %param.7) | copy-start | bytes 12292
  158.7 140.1 %all-gather.10.cloned.1.call-start = ((), (), s32[]{:S(2)}) async-start(), calls=%async_computation.3 | async-start | bytes 10485760 | tf_op jit(solution)/shard_map/all_gather | solution.py:53
  236.9 287.2 %reduce-scatter.2.cloned.1.call-start = ((), (), s32[]{:S(2)}) async-start(), calls=%async_computation.4 | async-start | bytes 17301504 | tf_op jit(solution)/shard_map/reduce_scatter | solution.py:61
  320.7 25.1 %all-to-all-start = ((f32[32,1,4096]{2,1,0:T(1,128)}), f32[32,1,4096]{2,1,0:T(1,128)S(1)}, u32[]{:S(2)}, u32[]{:S(2)}) async-start(f32[32,1,4096]{2,1,0:T(1,128)} %broadcast_in_dim.2), calls=%async_computation.1 | async-start | bytes 1048576 | tf_op jit(solution)/shard_map/all_to_all | solution.py:32
  346.2 179.8 %copy-start = (f32[1024]{0:T(1024)}, f32[1024]{0:T(1024)S(1)}, u32[]{:S(2)}) copy-start(f32[1024]{0:T(1024)S(1)} %dynamic_slice.7) | copy-start | bytes 12292
Sparse Core Ops, SparseCore 0:
  18.0 33.0 all-gather.11
  52.8 82.8 all-gather.13
  158.8 63.2 all-gather.7
  237.0 61.6 all-gather.9
  315.0 209.0 reduce-scatter.1
where the time goes:
time: 533 us
  waiting for transfers between devices  438 us (82%)
  matrix products  45.6 us (9%)
  between operations  13.8 us (3%)
  blocking collectives  10.6 us (2%)
  local copies, waits for them, and re-layouts  9.51 us (2%)
  starting transfers between devices  7.64 us (1%)
  other arithmetic  6.96 us (1%)
    reduce_scatter x1, waiting for transfers between devices, on_device(): lax.psum_scatter(lax.dot_general(gathered, pnl, (((0,), (0,)), ((), ())),...  178 us
    all_gather x2, waiting for transfers between devices, gather_in_order(): tiles = lax.all_gather(tiles, axes[k])  118 us
    all_gather x1, waiting for transfers between devices, on_device(): lax.all_gather(shocks, 'fac', axis=1, tiled=True)  63.4 us
    all_gather x1, waiting for transfers between devices, on_device(): gathered = lax.all_gather(pnl, 'fac', axis=1, tiled=True)  61.6 us
    all_to_all x1, waiting for transfers between devices, from_everyone(): return lax.all_to_all(copies, axis, split_axis=0, concat_axis=0, tiled=True)  17.8 us
    dot_general x1, matrix products, on_device(): lax.dot_general(gathered, pnl, (((0,), (0,)), ((), ())), preferred_elemen...  16.1 us
    dot_general x1, matrix products, on_device(): lax.dot_general(lax.all_gather(shocks, 'fac', axis=1, tiled=True), exposu...  14.8 us
    dot_general x1, matrix products, on_device(): jnp.dot(scenario_draws, whole_of(cholesky, SCEN, (1, 0, 2), 0), preferred...  14.7 us
  transfers between devices with their start and end apart: 6, of which 6 were waited for; matrix products, arithmetic and copies ran while one was open for 1% of the time, Pallas kernels for 0%

commit v1 on v0

--- a/solution.py
+++ b/solution.py
@@ -1,3 +1,4 @@
+import functools
 import jax
 import jax.numpy as jnp
 from jax import lax
@@ -5,6 +6,13 @@
 from jax.sharding import PartitionSpec as P
 
 SCEN = ("scen_0", "scen_1", "scen_2")
+
+
+def recast_joints(xx, axis_name):
+    return jnp.concatenate(lax.all_gather(xx, axis_name), 1)
+
+
+process_view_for = functools.partial(recast_joints, axis_name="fac")
 
 
 def in_order(tiles, dim):
@@ -50,7 +58,7 @@
         preferred_element_type=jnp.float32,
     )
     pnl = pnl_acc.astype(jnp.bfloat16)
-    gathered = lax.all_gather(pnl, "fac", axis=1, tiled=True)
+    gathered = process_view_for(pnl)
     desk_total = gathered.shape[1]
     column_sums = over_copies(jnp.sum(gathered, axis=0, dtype=jnp.float32), SCEN)
     scenario_total = count_rows * lax.axis_size(SCEN)

time: 533 us -> 543 us (1.019)
  local copies, waits for them, and re-layouts: 9.51 us -> 21.1 us
    all_gather x0 -> x1, local copies, waits for them, and re-layouts: none -> 11.6 us  [recast_joints(): return jnp.concatenate(lax.all_gather(xx, axis_name), 1)]
where the time goes in v1:
time: 543 us
  waiting for transfers between devices  439 us (81%)
  matrix products  43.9 us (8%)
  local copies, waits for them, and re-layouts  21.1 us (4%)
  between operations  13.8 us (3%)
  blocking collectives  10.6 us (2%)
  starting transfers between devices  7.63 us (1%)
  other arithmetic  6.95 us (1%)
    reduce_scatter x1, waiting for transfers between devices, on_device(): lax.psum_scatter(lax.dot_general(gathered, pnl, (((0,), (0,)), ((), ())),...  178 us
    all_gather x2, waiting for transfers between devices, gather_in_order(): tiles = lax.all_gather(tiles, axes[k])  118 us
    all_gather x1, waiting for transfers between devices, on_device(): lax.all_gather(shocks, 'fac', axis=1, tiled=True)  63.4 us
    all_gather x1, waiting for transfers between devices, recast_joints(): return jnp.concatenate(lax.all_gather(xx, axis_name), 1)  61.6 us
    all_to_all x1, waiting for transfers between devices, from_everyone(): return lax.all_to_all(copies, axis, split_axis=0, concat_axis=0, tiled=True)  17.8 us
    dot_general x1, matrix products, on_device(): jnp.dot(scenario_draws, whole_of(cholesky, SCEN, (1, 0, 2), 0), preferred...  14.7 us
    dot_general x1, matrix products, on_device(): lax.dot_general(lax.all_gather(shocks, 'fac', axis=1, tiled=True), exposu...  14.7 us
    dot_general x1, matrix products, on_device(): lax.dot_general(gathered, pnl, (((0,), (0,)), ((), ())), preferred_elemen...  14.5 us
  transfers between devices with their start and end apart: 6, of which 6 were waited for; matrix products, arithmetic and copies ran while one was open for 1% of the time, Pallas kernels for 0%

profile of v1, /device:TPU:0, one launch (start us, length us, event | category | flops | bytes accessed | tf_op | source)
XLA Modules:
  0.0 542.7 jit_solution(4538596407335264963)
XLA Ops:
  7.2 0.0 all-gather.11.cloned.1.call-start
  7.2 10.6 %all-gather = bf16[256,1024]{1,0:T(8,128)(2,1)} all-gather(bf16[128,1024]{1,0:T(8,128)(2,1)} %param.5), channel_id=2, replica_groups=mesh['scen_0'=4,'scen_1'=2,'scen_2'=4,'fac'=4] {'scen_1'}, dimensions={0}, use_global_device_ids=true | all-gather | bytes 786432 | tf_op jit(solution)/shard_map/all_gather | solution.py:27
  17.8 0.0 all-gather.11.cloned.1.call-update
  17.8 0.0 all-gather.13.cloned.1.call-start
  17.9 33.2 %all-gather.11.cloned.1.call-done = bf16[8,128,1024]{2,1,0:T(8,128)(2,1)} async-done(((bf16[2,128,1024]{2,1,0:T(8,128)(2,1)}), bf16[8,128,1024]{2,1,0:T(8,128)(2,1)}) %all-gather.11.cloned.1.call-update) | async-done | bytes 2097168 | tf_op jit(solution)/shard_map/all_gather | solution.py:27
  51.1 0.0 all-gather.13.cloned.1.call-update
  51.1 0.0 all-gather.9.cloned.1.call-start
  51.2 84.5 %all-gather.13.cloned.1.call-done = bf16[16,2,128,1024]{3,2,1,0:T(8,128)(2,1)} async-done(((bf16[4,2,128,1024]{3,2,1,0:T(8,128)(2,1)}), bf16[16,2,128,1024]{3,2,1,0:T(8,128)(2,1)}) %all-gather.13.cloned.1.call-update) | async-done | bytes 8388624 | tf_op jit(solution)/shard_map/all_gather | solution.py:27
  135.7 0.0 copy-start.2
  135.7 8.2 %copy.13 = bf16[4,2,4,128,1024]{4,3,2,1,0:T(8,128)(2,1)} copy(bf16[4,2,4,128,1024]{4,3,1,0,2:T(8,128)(2,1)} %bitcast.22) | data formatting | bytes 16777216 | tf_op jit(solution)/shard_map/transpose | solution.py:30
  143.9 0.0 copy-done.2
  143.9 14.7 %add_convert_fusion = bf16[1024,1024]{1,0:T(8,128)(2,1)} fusion(f32[1024]{0:T(1024)S(1)} %copy-done.2, bf16[1024,4096]{1,0:T(8,128)(2,1)} %param.4, bf16[4096,1024]{1,0:T(8,128)(2,1)} %bitcast.24), kind=kOutput, calls=%fused_computation.1 | convolution fusion | flops 8592031744 | bytes 18878464 | tf_op jit(solution)/shard_map/dot_general | solution.py:50
  158.6 0.0 all-gather.9.cloned.1.call-update
  158.7 0.0 all-gather.15.cloned.1.call-start
  158.7 63.4 %all-gather.9.cloned.1.call-done = bf16[1024,4096]{1,0:T(8,128)(2,1)} async-done(((bf16[1024,1024]{1,0:T(8,128)(2,1)}), bf16[1024,4096]{1,0:T(8,128)(2,1)}) %all-gather.9.cloned.1.call-update) | async-done | bytes 8388624 | tf_op jit(solution)/shard_map/all_gather | solution.py:55
  222.1 14.7 %convolution_convert_fusion = bf16[1024,1024]{1,0:T(8,128)(2,1)} fusion(bf16[1024,4096]{1,0:T(8,128)(2,1)} %all-gather.9.cloned.1.call-done, bf16[1024,4096]{1,0:T(8,128)(2,1)} %param.6), kind=kOutput, calls=%fused_computation.2 | convolution fusion | flops 8590983168 | bytes 18874368 | tf_op jit(solution)/shard_map/dot_general | solution.py:54
  236.8 0.0 all-gather.15.cloned.1.call-update
  236.9 0.2 reduce-scatter.2.cloned.1.call-start
  237.1 61.6 %all-gather.15.cloned.1.call-done = bf16[4096,1024]{1,0:T(8,128)(2,1)} async-done(((bf16[1024,1024]{1,0:T(8,128)(2,1)}), bf16[4096,1024]{1,0:T(8,128)(2,1)}) %all-gather.15.cloned.1.call-update) | async-done | bytes 8388624 | tf_op jit(solution)/shard_map/all_gather | solution.py:12
  298.7 0.0 copy-start
  298.7 11.6 %copy.14 = bf16[4,1024,1024]{1,2,0:T(8,128)(2,1)} copy(bf16[4,1024,1024]{2,1,0:T(8,128)(2,1)} %bitcast.23) | data formatting | bytes 16777216 | tf_op jit(solution)/shard_map/all_gather | solution.py:12
  310.3 0.0 copy-done
  310.3 14.5 %fusion = f32[4096,1024]{1,0:T(8,128)} fusion(bf16[1024,4096]{0,1:T(8,128)(2,1)} %bitcast.21, bf16[1024,1024]{1,0:T(8,128)(2,1)S(1)} %copy-done), kind=kOutput, calls=%fused_computation.7 | convolution fusion | flops 8589934592 | bytes 27262976 | tf_op jit(solution)/shard_map/dot_general | solution.py:70
  324.8 0.0 reduce-scatter.2.cloned.1.call-update
  324.8 4.6 convert_reduce_fusion
  329.4 1.3 broadcast_in_dim.9
  330.7 7.3 %all-to-all-start = ((f32[32,1,4096]{2,1,0:T(1,128)}), f32[32,1,4096]{2,1,0:T(1,128)S(1)}, u32[]{:S(2)}, u32[]{:S(2)}) async-start(f32[32,1,4096]{2,1,0:T(1,128)} %broadcast_in_dim.9), calls=%async_computation.1 | async-start | bytes 1048576 | tf_op jit(solution)/shard_map/all_to_all | solution.py:40
  337.9 17.8 %all-to-all-done = f32[32,1,4096]{2,1,0:T(1,128)S(1)} async-done(((f32[32,1,4096]{2,1,0:T(1,128)}), f32[32,1,4096]{2,1,0:T(1,128)S(1)}, u32[]{:S(2)}, u32[]{:S(2)}) %all-to-all-start) | async-done | bytes 524320 | tf_op jit(solution)/shard_map/all_to_all | solution.py:40
  355.7 0.4 reduce_sum.19
  356.1 0.0 copy-start.1
  356.1 0.1 dynamic-slice_multiply_fusion
  356.2 178.0 %reduce-scatter.2.cloned.1.call-done = f32[128,1024]{1,0:T(8,128)} async-done(((f32[4096,1024]{1,0:T(8,128)}), f32[128,1024]{1,0:T(8,128)}) %reduce-scatter.2.cloned.1.call-update) | async-done | bytes 524304 | tf_op jit(solution)/shard_map/reduce_scatter | solution.py:69
  534.2 2.0 subtract_multiply_fusion
  536.1 0.0 copy-done.1
  (3 shorter events, 0.0 us)
Async XLA Ops:
  7.2 43.9 %all-gather.11.cloned.1.call-start = ((), (), s32[]{:S(2)}) async-start(), calls=%async_computation.4 | async-start | bytes 2621440 | tf_op jit(solution)/shard_map/all_gather | solution.py:27
  17.8 117.8 %all-gather.13.cloned.1.call-start = ((), (), s32[]{:S(2)}) async-start(), calls=%async_computation.5 | async-start | bytes 10485760 | tf_op jit(solution)/shard_map/all_gather | solution.py:27
  51.1 171.0 %all-gather.9.cloned.1.call-start = ((), (), s32[]{:S(2)}) async-start(), calls=%async_computation.2 | async-start | bytes 10485760 | tf_op jit(solution)/shard_map/all_gather | solution.py:55
  135.7 8.2 %copy-start.2 = (f32[1024]{0:T(1024)S(1)}, f32[1024]{0:T(1024)}, u32[]{:S(2)}) copy-start(f32[1024]{0:T(1024)} %param.7) | copy-start | bytes 12292
  158.7 140.1 %all-gather.15.cloned.1.call-start = ((), (), s32[]{:S(2)}) async-start(), calls=%async_computation.6 | async-start | bytes 10485760 | tf_op jit(solution)/shard_map/all_gather | solution.py:12
  236.9 297.3 %reduce-scatter.2.cloned.1.call-start = ((), (), s32[]{:S(2)}) async-start(), calls=%async_computation.3 | async-start | bytes 17301504 | tf_op jit(solution)/shard_map/reduce_scatter | solution.py:69
  298.7 11.6 %copy-start = (bf16[1024,1024]{1,0:T(8,128)(2,1)S(1)}, bf16[1024,1024]{1,0:T(8,128)(2,1)}, u32[]{:S(2)}) copy-start(bf16[1024,1024]{1,0:T(8,128)(2,1)} %convolution_convert_fusion) | copy-start | bytes 6291460
  330.7 25.1 %all-to-all-start = ((f32[32,1,4096]{2,1,0:T(1,128)}), f32[32,1,4096]{2,1,0:T(1,128)S(1)}, u32[]{:S(2)}, u32[]{:S(2)}) async-start(f32[32,1,4096]{2,1,0:T(1,128)} %broadcast_in_dim.9), calls=%async_computation.1 | async-start | bytes 1048576 | tf_op jit(solution)/shard_map/all_to_all | solution.py:40
  356.1 180.0 %copy-start.1 = (f32[1024]{0:T(1024)}, f32[1024]{0:T(1024)S(1)}, u32[]{:S(2)}) copy-start(f32[1024]{0:T(1024)S(1)} %dynamic_slice.7) | copy-start | bytes 12292
Sparse Core Ops, SparseCore 0:
  18.0 33.0 all-gather.10
  52.7 82.8 all-gather.12
  158.8 63.2 all-gather.8
  237.0 61.7 all-gather.14
  325.0 209.1 reduce-scatter.1
